TPU v7x, 32 devices: a whole 2x2x4 slice. The times are simulated.
32 devices in a mesh: row: 8 (over y, x, core), col: 4 (over z).
Axes of the slice: x: 2, y: 2, z: 4, core: 2. Of those that a mesh axis runs over, the one named last changes fastest.
Arguments:
- a_window: float32 [16384, 4096], P('row', 'col'), may hold values from -6 to 6
- l_panel: float32 [16384, 1024], P('row'), may hold values from -0.1875 to 0.1875
- l_inverse: float32 [2, 512, 512], replicated, may hold values from -2 to 2, as said below
Outputs:
- reduced: float32 [16384, 4096], P('row', 'col')
Inputs may be any that keep to these rules, and one draw needn't show every extreme that they name: `l_inverse`: both blocks are lower triangular, with diagonal entries between 0.5 and 2.
All inputs are finite; a program needn't handle non-finite values.
Results may differ from a plain program's by a relative error of at most 0.000067.
Values sent between devices are 32-bit elements; how exact they have to be, the bound alone decides.
A program may use at most 128 MiB of HBM per device.

v0:
```python
import functools

import jax
import jax.numpy as jnp
from jax import lax
from jax.experimental import pallas as pl
from jax.experimental.pallas import tpu as pltpu
from jax.sharding import PartitionSpec as P

MESH = pl.DeviceIdType.MESH
SPAN = 16
TILE = 256
AHEAD = 8
LAG = 3
NN, NT = ((1,), (0,)), ((1,), (1,))
COUPLE, LOWER, TOP, TILEROWS = range(4)


def bits_of(count):
    return max(count.bit_length() - 1, 0)


def ring_pos(index, count):
    if count & (count - 1):
        return index
    parity, place = 0, 0
    for bit in reversed(range(bits_of(count))):
        parity = (parity + (index // 2**bit) % 2) % 2
        place = place + parity * 2**bit
    return place


def ring_at(place, count):
    if count & (count - 1):
        return place
    index = 0
    for bit in range(bits_of(count)):
        index = index + (((place // 2**bit) % 2 + (place // 2 ** (bit + 1)) % 2) % 2) * 2**bit
    return index


def seen_from(index, root, count):
    if count & (count - 1):
        return (index - root + count) % count
    return sum((((index // 2**bit) % 2 + (root // 2**bit) % 2) % 2) * 2**bit for bit in range(bits_of(count)))


def placed_from(offset, root, count):
    if count & (count - 1):
        return (offset + root) % count
    return seen_from(offset, root, count)


def split(value):
    high = value.astype(jnp.bfloat16)
    return high, (value - high.astype(jnp.float32)).astype(jnp.bfloat16)


def dot3(left_high, left_low, high, low, dims):
    total = lax.dot_general(left_high, high, (dims, ((), ())), preferred_element_type=jnp.float32)
    total += lax.dot_general(left_high, low, (dims, ((), ())), preferred_element_type=jnp.float32)
    return total + lax.dot_general(left_low, high, (dims, ((), ())), preferred_element_type=jnp.float32)


def full_dot(left, right):
    return lax.dot_general(
        left, right, (NN, ((), ())), precision=lax.Precision.HIGHEST, preferred_element_type=jnp.float32
    )


def step_kernel(
    rows_n, cols_n, a_ref, l_ref, i_ref, out_ref,
    zbuf, top, tile, low, couple, part, work, lh, ll, ih, il, kh, kl, ch, cl, vh, vl,
    zs, zr, cs, cr, ls, lr, ts, tr, gs, gr, here,
):
    row, col = lax.axis_index("row"), lax.axis_index("col")
    depth, width = a_ref.shape
    half = i_ref.shape[1]
    pieces = depth // SPAN
    top_pieces = width // SPAN
    tile_n = min(TILE, width)
    blocks, groups = depth // tile_n, width // tile_n
    per_block = tile_n // SPAN
    small = min(128, half)
    panel = col == 0
    relays = jnp.logical_and(col != 0, col != cols_n - 1)
    root = (col * width) // depth
    offset = (col * width) % depth
    pair = 2 if rows_n % 2 == 0 else 1
    chain = rows_n // pair
    most = chain - 1 + pair - 1
    f32 = jnp.float32

    low_rows = 2 * SPAN
    items = (
        (couple, cs, cr, half // 2, 2, 0, 0),
        (low, ls, lr, low_rows, width // low_rows, root, 0),
        (top, ts, tr, SPAN, top_pieces, 0, 0),
        (tile, gs, gr, SPAN, top_pieces, root, offset // SPAN),
    )

    def rel(item):
        return seen_from(row, items[item][5], rows_n)

    def place(item):
        return ring_pos(rel(item) // pair, chain)

    def far(item, way):
        at = place(item)
        return at if way == 0 else (chain - at) % chain

    def p_copy(item, kind, at, view, target):
        buffer, send, recv, count = items[item][:4]
        return pltpu.make_async_remote_copy(
            src_ref=view,
            dst_ref=buffer.at[pl.ds(at * count, count)],
            send_sem=send.at[kind, at],
            recv_sem=recv.at[at],
            device_id=(target, col),
            device_id_type=MESH,
        )

    def p_next(item, way):
        at = (place(item) + (1 if way == 0 else chain - 1)) % chain
        return placed_from(ring_at(at, chain) * pair, items[item][5], rows_n)

    def p_twin(item):
        return placed_from(rel(item) + pair - 1, items[item][5], rows_n)

    def p_held(item, at):
        buffer, count = items[item][0], items[item][3]
        return buffer.at[pl.ds(at * count, count)]

    def p_send(item, way, at, view):
        if chain > 1:
            @pl.when(far(item, way) != chain - 1)
            def _():
                p_copy(item, 0, at, view, p_next(item, way)).start()

        if pair > 1:
            p_copy(item, 1, at, view, p_twin(item)).start()

    def p_first(item, way, at):
        count = items[item][3]
        if item == COUPLE:
            p_send(item, way, at, l_ref.at[pl.ds(half + at * count, count), pl.ds(0, half)])
        elif item == LOWER:
            p_send(item, way, at, l_ref.at[pl.ds(offset + at * count, count)])
        elif item == TOP:
            @pl.when(panel)
            def _():
                p_send(item, way, at, a_ref.at[pl.ds(at * count, count)])

            @pl.when(jnp.logical_not(panel))
            def _():
                p_send(item, way, at, top.at[pl.ds(at * count, count)])
        else:
            p_send(item, way, at, zbuf.at[pl.ds(offset + at * count, count)])

    def wanted(item):
        return col != 0 if item in (LOWER, TILEROWS) else col >= 0

    def p_step(item, i):
        count, start = items[item][4], items[item][6]
        for way in range(2):
            stage = far(item, way) + rel(item) % pair
            at = i - start - stage * LAG

            @pl.when(
                jnp.logical_and(wanted(item), jnp.logical_and(jnp.logical_and(at >= 0, at < count), at % 2 == way))
            )
            def _():
                @pl.when(rel(item) == 0)
                def _():
                    p_first(item, way, at)

                @pl.when(rel(item) != 0)
                def _():
                    p_copy(item, 0, at, p_held(item, at), row).wait_recv()

                    @pl.when(rel(item) % pair == 0)
                    def _():
                        p_send(item, way, at, p_held(item, at))

    def p_finish(item):
        count = items[item][4]

        @pl.when(jnp.logical_and(wanted(item), rel(item) % pair == 0))
        def _():
            @pl.loop(0, count)
            def _(at):
                for way in range(2):
                    if chain > 1:
                        @pl.when(jnp.logical_and(at % 2 == way, far(item, way) != chain - 1))
                        def _():
                            p_copy(item, 0, at, p_held(item, at), row).wait_send()

                if pair > 1:
                    p_copy(item, 1, at, p_held(item, at), row).wait_send()

    def z_copy(i, source, target):
        return pltpu.make_async_remote_copy(
            src_ref=source.at[pl.ds(i * SPAN, SPAN)],
            dst_ref=target.at[pl.ds(i * SPAN, SPAN)],
            send_sem=zs.at[i],
            recv_sem=zr.at[i],
            device_id=(row, jnp.minimum(col + 1, cols_n - 1)),
            device_id_type=MESH,
        )

    def z_first(i):
        is_top = jnp.logical_and(row == 0, i < top_pieces)

        @pl.when(is_top)
        def _():
            z_copy(i, a_ref, top).start()

        @pl.when(jnp.logical_not(is_top))
        def _():
            z_copy(i, a_ref, zbuf).start()

    def z_step(i):
        is_top = jnp.logical_and(row == 0, i < top_pieces)

        @pl.when(panel)
        def _():
            z_copy(i, a_ref, zbuf).wait_send()

            @pl.when(i + AHEAD < pieces)
            def _():
                z_first(i + AHEAD)

        for mine, buffer in ((is_top, top), (jnp.logical_not(is_top), zbuf)):
            @pl.when(jnp.logical_and(col != 0, mine))
            def _():
                z_copy(i, buffer, buffer).wait_recv()

                @pl.when(relays)
                def _():
                    z_copy(i, buffer, buffer).start()

    def l_load(b):
        return pltpu.make_async_copy(
            l_ref.at[pl.ds(b * tile_n, tile_n)], out_ref.at[pl.ds(b * tile_n, tile_n)], here.at[b]
        )

    def base_load(b):
        return pltpu.make_async_copy(
            a_ref.at[pl.ds(b * tile_n, tile_n)], out_ref.at[pl.ds(b * tile_n, tile_n)], here.at[blocks + b]
        )

    def a_load(b):
        return pltpu.make_async_copy(
            a_ref.at[pl.ds(b * tile_n, tile_n)], zbuf.at[pl.ds(b * tile_n, tile_n)], here.at[2 * blocks + b]
        )

    extra = 3 * blocks
    inv_load = [
        pltpu.make_async_copy(
            i_ref.at[k], work.at[pl.ds(k * half, half), pl.ds(k * half, half)], here.at[extra + k]
        )
        for k in range(2)
    ]
    couple_load = pltpu.make_async_copy(l_ref.at[pl.ds(half, half), pl.ds(0, half)], couple, here.at[extra + 2])
    low_load = pltpu.make_async_copy(l_ref.at[pl.ds(offset, width)], low, here.at[extra + 3])
    top_load = pltpu.make_async_copy(a_ref.at[pl.ds(0, width)], top, here.at[extra + 4])
    is_root = jnp.logical_and(row == root, col != 0)
    first_top = jnp.logical_and(row == 0, panel)

    for copy in inv_load:
        copy.start()

    @pl.loop(0, blocks)
    def _(b):
        l_load(b).start()

    barrier = pltpu.get_barrier_semaphore()
    for step in range(1, rows_n):
        pl.semaphore_signal(barrier, inc=1, device_id=((row + step) % rows_n, col), device_id_type=MESH)

    @pl.when(col != cols_n - 1)
    def _():
        pl.semaphore_signal(
            barrier, inc=1, device_id=(row, jnp.minimum(col + 1, cols_n - 1)), device_id_type=MESH
        )

    @pl.when(col != 0)
    def _():
        pl.semaphore_signal(barrier, inc=1, device_id=(row, jnp.maximum(col - 1, 0)), device_id_type=MESH)

    ends = jnp.where(col == 0, 1, 0) + jnp.where(col == cols_n - 1, 1, 0)
    pl.semaphore_wait(barrier, rows_n + 1 - ends)

    if cols_n > 1:
        @pl.when(panel)
        def _():
            @pl.loop(0, min(AHEAD, pieces))
            def _(i):
                z_first(i)

    @pl.when(row == 0)
    def _():
        couple_load.start()

    @pl.when(is_root)
    def _():
        low_load.start()

    @pl.when(first_top)
    def _():
        top_load.start()

    @pl.when(panel)
    def _():
        @pl.loop(0, blocks)
        def _(b):
            a_load(b).start()

    def minus_eye(at, count):
        rows = lax.broadcasted_iota(jnp.int32, (count, width), 0) + at
        columns = lax.broadcasted_iota(jnp.int32, (count, width), 1)
        return jnp.where(rows == columns, -1.0, 0.0)

    strip = min(64, tile_n)
    strips = depth // strip

    def l_piece(i):
        per = tile_n // strip
        b = i // per
        rows = pl.ds(pl.multiple_of(i * strip, strip), strip)
        block = pl.ds(pl.multiple_of(b * tile_n, tile_n), tile_n)

        @pl.when(i % per == 0)
        def _():
            l_load(b).wait()

        is_top = jnp.logical_and(row == 0, i * strip < width)

        @pl.when(is_top)
        def _():
            lh[rows] = jnp.where(panel, minus_eye(i * strip, strip), 0.0).astype(jnp.bfloat16)
            ll[rows] = jnp.zeros((strip, width), jnp.bfloat16)

        @pl.when(jnp.logical_not(is_top))
        def _():
            lh[rows], ll[rows] = split(out_ref[rows])

        @pl.when(i % per == per - 1)
        def _():
            @pl.when(panel)
            def _():
                out_ref[block] = jnp.zeros((tile_n, width), f32)

            @pl.when(jnp.logical_not(panel))
            def _():
                base_load(b).start()

    def corner_piece(k):
        count = half // small

        @pl.when(k == 0)
        def _():
            for copy in inv_load:
                copy.wait()

            @pl.when(row == 0)
            def _():
                couple_load.wait()

            work[0:half, half:] = jnp.zeros((half, width - half), f32)

        rows = pl.ds(pl.multiple_of((k % count) * small, small), small)
        lower_rows = pl.ds(pl.multiple_of(half + (k % count) * small, small), small)

        @pl.when(k < count)
        def _():
            part[rows] = full_dot(couple[rows], work[0:half, 0:half])

        @pl.when(k >= count)
        def _():
            work[lower_rows, 0:half] = -full_dot(work[lower_rows, half:], part[...])

    def rows_of(b):
        return pl.ds(pl.multiple_of(b * tile_n, tile_n), tile_n)

    def inv_piece(b):
        ih[rows_of(b)], il[rows_of(b)] = split(work[rows_of(b)])

    def key_piece(b):
        @pl.when(b == 0)
        def _():
            @pl.when(is_root)
            def _():
                low_load.wait()

            @pl.loop(0, blocks)
            def _(k):
                @pl.when(jnp.logical_not(panel))
                def _():
                    base_load(k).wait()

                @pl.when(panel)
                def _():
                    a_load(k).wait()

        @pl.when(panel)
        def _():
            low[rows_of(b)] = minus_eye(b * tile_n, tile_n)

        for n in range(groups):
            at = n * tile_n
            columns = slice(at, at + tile_n)
            high, rest = split(low[rows_of(b), at:])
            kh[rows_of(b), columns], kl[rows_of(b), columns] = split(
                dot3(high, rest, ih[at:, columns], il[at:, columns], NN)
            )

    def row_piece(h):
        b, side = h // 2, h % 2

        @pl.when(jnp.logical_not(jnp.logical_and(row == 0, b * tile_n < width)))
        def _():
            columns = pl.ds(pl.multiple_of(side * (width // 2), width // 2), width // 2)
            high, rest = split(zbuf[rows_of(b)])
            out_ref[rows_of(b), columns] -= dot3(high, rest, kh[columns], kl[columns], NT)

    def top_piece(b):
        @pl.when(jnp.logical_and(first_top, b == 0))
        def _():
            top_load.wait()

        ch[rows_of(b)], cl[rows_of(b)] = split(top[rows_of(b)])

    def product_piece(h):
        b, side = h // 2, h % 2
        columns = pl.ds(pl.multiple_of(side * (width // 2), width // 2), width // 2)
        high, rest = kh[rows_of(b)], kl[rows_of(b)]
        work[rows_of(b), columns] = dot3(high, rest, ch[columns], cl[columns], NT)

        @pl.when(jnp.logical_not(panel))
        def _():
            work[rows_of(b), columns] = 0.5 * (
                work[rows_of(b), columns] + dot3(high, rest, ch[:, columns], cl[:, columns], NN)
            )

    def weight_piece(j):
        own = pl.ds(pl.multiple_of((offset + j * tile_n) % depth, tile_n), tile_n)
        mine = jnp.where(row == root, zbuf[own], tile[rows_of(j)])
        high, rest = split(jnp.where(panel, 0.0, mine) - work[rows_of(j)])
        for n in range(groups):
            at, end = n * tile_n, (n + 1) * tile_n
            vh[:, at:end], vl[:, at:end] = split(
                dot3(high[:, :end], rest[:, :end], ih[at:end, :end], il[at:end, :end], NT)
            )

    big = min(2 * tile_n, depth)

    def column_piece(j, k):
        rows = pl.ds(pl.multiple_of(k * big, big), big)
        columns = pl.ds(pl.multiple_of(j * tile_n, tile_n), tile_n)
        out_ref[rows, columns] -= dot3(lh[rows], ll[rows], vh[...], vl[...], NT)

    corner_at = 2 + most * LAG
    corner_n = 2 * (half // small)
    inv_at = corner_at + corner_n
    key_at = max(inv_at + groups, width // low_rows + most * LAG, strips)
    row_at = key_at + groups
    caught = 0
    while caught < blocks and per_block * (caught + 1) <= row_at + 2 * caught:
        caught += 1
    top_at = max(row_at + 2 * caught, top_pieces + most * LAG)
    product_at = top_at + groups
    weight_from = product_at + 2 * groups
    column_n = depth // big
    tile_from = offset // SPAN + most * LAG
    last_tile = (depth - width) // SPAN + most * LAG
    window = 1 + column_n
    weight_starts = [
        jnp.maximum(weight_from + window * j, tile_from + per_block * (j + 1)) for j in range(groups)
    ]
    steps = max(
        pieces + 2,
        max(weight_from + window * (groups - 1), last_tile + per_block * groups) + window,
        top_at + groups,
    )

    def between(i, start, count):
        return jnp.logical_and(i >= start, i < start + count)

    @pl.loop(0, steps)
    def _(i):
        if cols_n > 1:
            @pl.when(i < pieces)
            def _():
                z_step(i)

        if rows_n > 1:
            for item in range(4):
                p_step(item, i)

        for start, count, piece in (
            (0, strips, l_piece),
            (corner_at, corner_n, corner_piece),
            (inv_at, groups, inv_piece),
            (key_at, groups, key_piece),
            (top_at, groups, top_piece),
            (product_at, 2 * groups, product_piece),
        ):
            @pl.when(between(i, start, count))
            def _(start=start, piece=piece):
                piece(i - start)

        late = i // per_block - 1
        early = between(i, row_at, 2 * caught)
        in_time = jnp.logical_and(i % per_block < 2, jnp.logical_and(late >= caught, late < blocks))

        @pl.when(jnp.logical_or(early, in_time))
        def _():
            row_piece(jnp.where(early, i - row_at, 2 * late + i % per_block))

        group, at, busy = 0, 0, 0
        for j in range(groups):
            mine = between(i, weight_starts[j], window)
            group = group + jnp.where(mine, j, 0)
            at = at + jnp.where(mine, i - weight_starts[j], 0)
            busy = busy + jnp.where(mine, 1, 0)

        @pl.when(jnp.logical_and(busy > 0, at == 0))
        def _():
            weight_piece(group)

        @pl.when(jnp.logical_and(busy > 0, at > 0))
        def _():
            column_piece(group, at - 1)

    if cols_n > 1:
        @pl.when(relays)
        def _():
            @pl.loop(0, pieces)
            def _(i):
                z_copy(i, zbuf, zbuf).wait_send()

    if rows_n > 1:
        for item in range(4):
            p_finish(item)


def body(rows_n, cols_n, a_window, l_panel, l_inverse):
    depth, width = a_window.shape
    half = l_inverse.shape[1]
    f32, bf16 = jnp.float32, jnp.bfloat16
    tile_n = min(TILE, width)
    dma = pltpu.SemaphoreType.DMA
    pieces, top_pieces, low_pieces = depth // SPAN, width // SPAN, width // (2 * SPAN)
    square = pltpu.VMEM((width, width), f32)
    narrow = pltpu.VMEM((width, width), bf16)
    return pl.pallas_call(
        functools.partial(step_kernel, rows_n, cols_n),
        out_shape=pltpu.VMEM((depth, width), f32),
        in_specs=[pl.BlockSpec(memory_space=pl.ANY)] * 3,
        out_specs=pl.BlockSpec(memory_space=pltpu.VMEM),
        scratch_shapes=[
            pltpu.VMEM((depth, width), f32),
            square,
            square,
            square,
            pltpu.VMEM((half, half), f32),
            pltpu.VMEM((half, half), f32),
            square,
            pltpu.VMEM((depth, width), bf16),
            pltpu.VMEM((depth, width), bf16),
            narrow,
            narrow,
            narrow,
            narrow,
            narrow,
            narrow,
            pltpu.VMEM((tile_n, width), bf16),
            pltpu.VMEM((tile_n, width), bf16),
            dma((pieces,)),
            dma((pieces,)),
            dma((2, 2)),
            dma((2,)),
            dma((2, low_pieces)),
            dma((low_pieces,)),
            dma((2, top_pieces)),
            dma((top_pieces,)),
            dma((2, top_pieces)),
            dma((top_pieces,)),
            dma((3 * (depth // tile_n) + 5,)),
        ],
        compiler_params=pltpu.CompilerParams(
            collective_id=0, has_side_effects=True, vmem_limit_bytes=50 * 1024 * 1024
        ),
    )(a_window, l_panel, l_inverse)


def solution(mesh):
    placed = (P("row", "col"), P("row", None), P())
    return jax.shard_map(
        functools.partial(body, mesh.shape["row"], mesh.shape["col"]),
        mesh=mesh,
        in_specs=placed,
        out_specs=P("row", "col"),
        check_vma=False,
    )
```

profile of v0, /device:TPU:27, one launch (start us, length us, event | category | flops | bytes accessed | tf_op | source)
XLA Modules:
  0.0 242.4 jit_solution(7794946420795300190)
XLA Ops:
  0.0 239.0 %shard_map.37 = f32[2048,1024]{1,0:T(8,128)S(1)} custom-call(f32[2048,1024]{1,0:T(8,128)} %a_ref.1, f32[2048,1024]{1,0:T(8,128)} %l_ref.1, f32[2,512,512]{2,1,0:T(8,128)} %i_ref.1), custom_call_target="tpu_custom_call" | custom-call | tf_op jit(solution)/shard_map/pallas_call | solution.py:557
  239.0 3.4 %copy.5 = f32[2048,1024]{1,0:T(8,128)} copy(f32[2048,1024]{1,0:T(8,128)S(1)} %shard_map.37) | data formatting | bytes 16777216
where the time goes:
time: 244 us; the launch traced here: 242 us
  Pallas kernels  239 us (98%)
  local copies, waits for them, and re-layouts  3.4 us (1%)
    pallas_call x1, Pallas kernels, body(): pl.pallas_call(functools.partial(step_kernel, rows_n, cols_n), out_shape=...  239 us

commit v1 on v0

--- a/solution.py
+++ b/solution.py
@@ -9,9 +9,12 @@
 
 MESH = pl.DeviceIdType.MESH
 SPAN = 16
+PACE = 2
 TILE = 256
-AHEAD = 8
-LAG = 3
+AHEAD = (2, 16)
+LAGS = (4, 4, 4, 3)
+LATER = (0, 4, 0, 36)
+WAITS = (6, 6, 6, -8, -6)
 NN, NT = ((1,), (0,)), ((1,), (1,))
 COUPLE, LOWER, TOP, TILEROWS = range(4)
 
@@ -49,6 +52,10 @@
     if count & (count - 1):
         return (offset + root) % count
     return seen_from(offset, root, count)
+
+
+def couple_parts(half):
+    return max(half // (2 * PACE * SPAN), 2)
 
 
 def split(value):
@@ -88,156 +95,219 @@
     offset = (col * width) % depth
     pair = 2 if rows_n % 2 == 0 else 1
     chain = rows_n // pair
-    most = chain - 1 + pair - 1
     f32 = jnp.float32
 
-    low_rows = 2 * SPAN
+    low_rows, own_rows = 2 * PACE * SPAN, PACE * SPAN
+    parts = couple_parts(half)
+    natural = row == 0
+    turned = depth // width - 1 - offset // width
+    tile_at = jnp.where(root == 0, offset // width, turned) * top_pieces
+    tile_start = jnp.where(tile_at > 0, tile_at, LATER[TILEROWS])
+
+    def sent_at(index, per):
+        return jnp.where(natural, index, (depth // width - 1 - index // per) * per + index % per)
+
     items = (
-        (couple, cs, cr, half // 2, 2, 0, 0),
-        (low, ls, lr, low_rows, width // low_rows, root, 0),
-        (top, ts, tr, SPAN, top_pieces, 0, 0),
-        (tile, gs, gr, SPAN, top_pieces, root, offset // SPAN),
+        (couple, cs, cr, half // parts, parts, 0, 0),
+        (low, ls, lr, low_rows, width // low_rows, root, LATER[LOWER]),
+        (top, ts, tr, own_rows, width // own_rows, 0, PACE - 1),
+        (tile, gs, gr, own_rows, width // own_rows, root, tile_start + PACE - 1),
     )
 
-    def rel(item):
-        return seen_from(row, items[item][5], rows_n)
-
-    def place(item):
-        return ring_pos(rel(item) // pair, chain)
-
-    def far(item, way):
-        at = place(item)
-        return at if way == 0 else (chain - at) % chain
-
-    def p_copy(item, kind, at, view, target):
+    rel, far, is_last, level, p_next, p_twin = [], [], [], [], [], []
+    for item in range(4):
+        origin = items[item][5]
+        seen = seen_from(row, origin, rows_n)
+        at = ring_pos(seen // pair, chain)
+        odd = seen % pair
+        ways = (at, (chain - at) % chain)
+        short = item == TILEROWS and chain > 2
+        rel.append(seen)
+        far.append(ways)
+        is_last.append(tuple(way >= chain - (2 if short else 1) for way in ways))
+        if item == TILEROWS:
+            ways = tuple(jnp.where(way == chain - 1, jnp.minimum(way, 1), way) for way in ways)
+        level.append(tuple(way + odd for way in ways))
+        p_next.append(
+            tuple(
+                placed_from(ring_at((at + (1 if way == 0 else chain - 1)) % chain, chain) * pair, origin, rows_n)
+                for way in range(2)
+            )
+        )
+        p_twin.append(placed_from(seen + (pair - 1) * (1 - odd), origin, rows_n))
+
+    def wait(item):
+        if item != TILEROWS:
+            return WAITS[item]
+        return jnp.where(tile_at > 0, jnp.where(root == 0, WAITS[item], WAITS[item + 1]), 0)
+
+    begins = [
+        tuple(items[item][6] + jnp.where(of_way > 0, of_way * LAGS[item] + wait(item), 0) for of_way in level[item])
+        for item in range(4)
+    ]
+    sends_on = [rel[item] % pair == 0 for item in range(4)]
+    is_first = [rel[item] == 0 for item in range(4)]
+
+    def most(item):
+        chips = max(chain - 2, 1) if item == TILEROWS and chain > 1 else chain - 1
+        return chips + pair - 1
+
+    def p_copy(item, kind, at, source, first, columns, target):
         buffer, send, recv, count = items[item][:4]
         return pltpu.make_async_remote_copy(
-            src_ref=view,
-            dst_ref=buffer.at[pl.ds(at * count, count)],
+            src_ref=source.at[pl.ds(first + at * count, count), columns],
+            dst_ref=buffer.at[pl.ds(at * count, count), columns],
             send_sem=send.at[kind, at],
             recv_sem=recv.at[at],
             device_id=(target, col),
             device_id_type=MESH,
         )
 
-    def p_next(item, way):
-        at = (place(item) + (1 if way == 0 else chain - 1)) % chain
-        return placed_from(ring_at(at, chain) * pair, items[item][5], rows_n)
-
-    def p_twin(item):
-        return placed_from(rel(item) + pair - 1, items[item][5], rows_n)
-
-    def p_held(item, at):
-        buffer, count = items[item][0], items[item][3]
-        return buffer.at[pl.ds(at * count, count)]
-
-    def p_send(item, way, at, view):
+    def upper(k):
+        return pl.ds(k * tile_n, width - k * tile_n)
+
+    def each(item, at, act):
+        if item != TOP:
+            act(pl.ds(0, items[item][0].shape[1]))
+            return
+
+        @pl.when(panel)
+        def _():
+            act(pl.ds(0, width))
+
+        for k in range(groups):
+            @pl.when(jnp.logical_and(jnp.logical_not(panel), at // (tile_n // own_rows) == k))
+            def _(k=k):
+                act(upper(k))
+
+    def p_send(item, way, at, source, first, columns):
         if chain > 1:
-            @pl.when(far(item, way) != chain - 1)
-            def _():
-                p_copy(item, 0, at, view, p_next(item, way)).start()
+            @pl.when(jnp.logical_not(is_last[item][way]))
+            def _():
+                p_copy(item, 0, at, source, first, columns, p_next[item][way]).start()
+
+        if chain > 2 and item == TILEROWS:
+            @pl.when(is_first[item])
+            def _():
+                p_copy(item, 2, at, source, first, columns, p_next[item][1 - way]).start()
 
         if pair > 1:
-            p_copy(item, 1, at, view, p_twin(item)).start()
-
-    def p_first(item, way, at):
-        count = items[item][3]
+            p_copy(item, 1, at, source, first, columns, p_twin[item]).start()
+
+    def p_first(item, way, at, columns):
         if item == COUPLE:
-            p_send(item, way, at, l_ref.at[pl.ds(half + at * count, count), pl.ds(0, half)])
+            p_send(item, way, at, l_ref, half, columns)
         elif item == LOWER:
-            p_send(item, way, at, l_ref.at[pl.ds(offset + at * count, count)])
+            p_send(item, way, at, l_ref, offset, columns)
         elif item == TOP:
             @pl.when(panel)
             def _():
-                p_send(item, way, at, a_ref.at[pl.ds(at * count, count)])
+                p_send(item, way, at, a_ref, 0, columns)
 
             @pl.when(jnp.logical_not(panel))
             def _():
-                p_send(item, way, at, top.at[pl.ds(at * count, count)])
+                p_send(item, way, at, top, 0, columns)
         else:
-            p_send(item, way, at, zbuf.at[pl.ds(offset + at * count, count)])
-
-    def wanted(item):
-        return col != 0 if item in (LOWER, TILEROWS) else col >= 0
+            p_send(item, way, at, zbuf, offset, columns)
+
+    wanted = [col != 0 if item in (LOWER, TILEROWS) else col >= 0 for item in range(4)]
 
     def p_step(item, i):
-        count, start = items[item][4], items[item][6]
+        count = items[item][4]
         for way in range(2):
-            stage = far(item, way) + rel(item) % pair
-            at = i - start - stage * LAG
+            since = i - begins[item][way]
+            at = since // PACE
 
             @pl.when(
-                jnp.logical_and(wanted(item), jnp.logical_and(jnp.logical_and(at >= 0, at < count), at % 2 == way))
+                jnp.logical_and(wanted[item], jnp.logical_and(jnp.logical_and(since >= 0, at < count), since % (2 * PACE) == way * PACE))
             )
             def _():
-                @pl.when(rel(item) == 0)
-                def _():
-                    p_first(item, way, at)
-
-                @pl.when(rel(item) != 0)
-                def _():
-                    p_copy(item, 0, at, p_held(item, at), row).wait_recv()
-
-                    @pl.when(rel(item) % pair == 0)
+                def act(columns):
+                    @pl.when(is_first[item])
                     def _():
-                        p_send(item, way, at, p_held(item, at))
+                        p_first(item, way, at, columns)
+
+                    @pl.when(jnp.logical_not(is_first[item]))
+                    def _():
+                        buffer = items[item][0]
+                        p_copy(item, 0, at, buffer, 0, columns, row).wait_recv()
+
+                        @pl.when(sends_on[item])
+                        def _():
+                            p_send(item, way, at, buffer, 0, columns)
+
+                each(item, at, act)
 
     def p_finish(item):
-        count = items[item][4]
-
-        @pl.when(jnp.logical_and(wanted(item), rel(item) % pair == 0))
+        buffer, count = items[item][0], items[item][4]
+
+        @pl.when(jnp.logical_and(wanted[item], sends_on[item]))
         def _():
             @pl.loop(0, count)
             def _(at):
-                for way in range(2):
-                    if chain > 1:
-                        @pl.when(jnp.logical_and(at % 2 == way, far(item, way) != chain - 1))
+                def act(columns):
+                    for way in range(2):
+                        if chain > 1:
+                            @pl.when(jnp.logical_and(at % 2 == way, jnp.logical_not(is_last[item][way])))
+                            def _():
+                                p_copy(item, 0, at, buffer, 0, columns, row).wait_send()
+
+                    if chain > 2 and item == TILEROWS:
+                        @pl.when(is_first[item])
                         def _():
-                            p_copy(item, 0, at, p_held(item, at), row).wait_send()
-
-                if pair > 1:
-                    p_copy(item, 1, at, p_held(item, at), row).wait_send()
-
-    def z_copy(i, source, target):
+                            p_copy(item, 2, at, buffer, 0, columns, row).wait_send()
+
+                    if pair > 1:
+                        p_copy(item, 1, at, buffer, 0, columns, row).wait_send()
+
+                each(item, at, act)
+
+    def z_copy(i, source, target, columns):
+        rows = pl.ds(pl.multiple_of(sent_at(i, top_pieces) * SPAN, SPAN), SPAN)
         return pltpu.make_async_remote_copy(
-            src_ref=source.at[pl.ds(i * SPAN, SPAN)],
-            dst_ref=target.at[pl.ds(i * SPAN, SPAN)],
+            src_ref=source.at[rows, columns],
+            dst_ref=target.at[rows, columns],
             send_sem=zs.at[i],
             recv_sem=zr.at[i],
             device_id=(row, jnp.minimum(col + 1, cols_n - 1)),
             device_id_type=MESH,
         )
 
+    def z_each(i, act):
+        is_top = jnp.logical_and(row == 0, i < top_pieces)
+        for k in range(groups):
+            @pl.when(jnp.logical_and(is_top, i // per_block == k))
+            def _(k=k):
+                act(tile, top, upper(k))
+
+        @pl.when(jnp.logical_not(is_top))
+        def _():
+            act(a_ref, zbuf, pl.ds(0, width))
+
+    ahead = jnp.where(row == 0, AHEAD[0], AHEAD[1])
+
     def z_first(i):
-        is_top = jnp.logical_and(row == 0, i < top_pieces)
-
-        @pl.when(is_top)
-        def _():
-            z_copy(i, a_ref, top).start()
-
-        @pl.when(jnp.logical_not(is_top))
-        def _():
-            z_copy(i, a_ref, zbuf).start()
+        z_each(i, lambda source, target, columns: z_copy(i, source, target, columns).start())
 
     def z_step(i):
-        is_top = jnp.logical_and(row == 0, i < top_pieces)
-
         @pl.when(panel)
         def _():
-            z_copy(i, a_ref, zbuf).wait_send()
-
-            @pl.when(i + AHEAD < pieces)
-            def _():
-                z_first(i + AHEAD)
-
-        for mine, buffer in ((is_top, top), (jnp.logical_not(is_top), zbuf)):
-            @pl.when(jnp.logical_and(col != 0, mine))
-            def _():
-                z_copy(i, buffer, buffer).wait_recv()
+            z_each(i, lambda source, target, columns: z_copy(i, source, target, columns).wait_send())
+
+            @pl.when(i + ahead < pieces)
+            def _():
+                z_first(i + ahead)
+
+        @pl.when(col != 0)
+        def _():
+            def act(source, target, columns):
+                z_copy(i, target, target, columns).wait_recv()
 
                 @pl.when(relays)
                 def _():
-                    z_copy(i, buffer, buffer).start()
+                    z_copy(i, target, target, columns).start()
+
+            z_each(i, act)
 
     def l_load(b):
         return pltpu.make_async_copy(
@@ -267,6 +337,10 @@
     is_root = jnp.logical_and(row == root, col != 0)
     first_top = jnp.logical_and(row == 0, panel)
 
+    @pl.when(first_top)
+    def _():
+        top_load.start()
+
     for copy in inv_load:
         copy.start()
 
@@ -291,10 +365,19 @@
     ends = jnp.where(col == 0, 1, 0) + jnp.where(col == cols_n - 1, 1, 0)
     pl.semaphore_wait(barrier, rows_n + 1 - ends)
 
+    @pl.when(first_top)
+    def _():
+        top_load.wait()
+        for k in range(groups):
+            rows = slice(k * tile_n, (k + 1) * tile_n)
+            for n in range(k, groups):
+                columns = slice(n * tile_n, (n + 1) * tile_n)
+                tile[rows, columns] = top[rows, columns] + top[columns, rows].T
+
     if cols_n > 1:
         @pl.when(panel)
         def _():
-            @pl.loop(0, min(AHEAD, pieces))
+            @pl.loop(0, jnp.minimum(ahead, pieces))
             def _(i):
                 z_first(i)
 
@@ -305,10 +388,6 @@
     @pl.when(is_root)
     def _():
         low_load.start()
-
-    @pl.when(first_top)
-    def _():
-        top_load.start()
 
     @pl.when(panel)
     def _():
@@ -416,7 +495,7 @@
             )
 
     def row_piece(h):
-        b, side = h // 2, h % 2
+        b, side = sent_at(h // 2, groups), h % 2
 
         @pl.when(jnp.logical_not(jnp.logical_and(row == 0, b * tile_n < width)))
         def _():
@@ -425,32 +504,36 @@
             out_ref[rows_of(b), columns] -= dot3(high, rest, kh[columns], kl[columns], NT)
 
     def top_piece(b):
-        @pl.when(jnp.logical_and(first_top, b == 0))
-        def _():
-            top_load.wait()
-
         ch[rows_of(b)], cl[rows_of(b)] = split(top[rows_of(b)])
 
     def product_piece(h):
-        b, side = h // 2, h % 2
-        columns = pl.ds(pl.multiple_of(side * (width // 2), width // 2), width // 2)
-        high, rest = kh[rows_of(b)], kl[rows_of(b)]
-        work[rows_of(b), columns] = dot3(high, rest, ch[columns], cl[columns], NT)
-
-        @pl.when(jnp.logical_not(panel))
-        def _():
-            work[rows_of(b), columns] = 0.5 * (
-                work[rows_of(b), columns] + dot3(high, rest, ch[:, columns], cl[:, columns], NN)
-            )
+        b, group = h // groups, h % groups
+        high, rest = kh.at[rows_of(b)], kl.at[rows_of(b)]
+        for n in range(groups):
+            own, at = slice(n * tile_n, (n + 1) * tile_n), (n + 1) * tile_n
+
+            @pl.when(jnp.logical_and(group == n, panel))
+            def _():
+                work[rows_of(b), own] = dot3(high[...], rest[...], ch[own], cl[own], NT)
+
+            @pl.when(jnp.logical_and(group == n, jnp.logical_not(panel)))
+            def _():
+                total = dot3(high[:, :at], rest[:, :at], ch[:at, own], cl[:at, own], NN)
+                if n + 1 < groups:
+                    total += dot3(high[:, at:], rest[:, at:], ch[own, at:], cl[own, at:], NT)
+                work[rows_of(b), own] = 0.5 * total
 
     def weight_piece(j):
         own = pl.ds(pl.multiple_of((offset + j * tile_n) % depth, tile_n), tile_n)
-        mine = jnp.where(row == root, zbuf[own], tile[rows_of(j)])
-        high, rest = split(jnp.where(panel, 0.0, mine) - work[rows_of(j)])
-        for n in range(groups):
+        for mine, source, rows in ((row == root, zbuf, own), (row != root, tile, rows_of(j))):
+            @pl.when(mine)
+            def _(source=source, rows=rows):
+                vh[...], vl[...] = split(jnp.where(panel, 0.0, source[rows]) - work[rows_of(j)])
+
+        for n in reversed(range(groups)):
             at, end = n * tile_n, (n + 1) * tile_n
             vh[:, at:end], vl[:, at:end] = split(
-                dot3(high[:, :end], rest[:, :end], ih[at:end, :end], il[at:end, :end], NT)
+                dot3(vh[:, :end], vl[:, :end], ih[at:end, :end], il[at:end, :end], NT)
             )
 
     big = min(2 * tile_n, depth)
@@ -460,20 +543,20 @@
         columns = pl.ds(pl.multiple_of(j * tile_n, tile_n), tile_n)
         out_ref[rows, columns] -= dot3(lh[rows], ll[rows], vh[...], vl[...], NT)
 
-    corner_at = 2 + most * LAG
+    corner_at = PACE * parts + most(COUPLE) * LAGS[COUPLE] + WAITS[COUPLE]
     corner_n = 2 * (half // small)
     inv_at = corner_at + corner_n
-    key_at = max(inv_at + groups, width // low_rows + most * LAG, strips)
+    key_at = max(inv_at + groups, LATER[LOWER] + PACE * (width // low_rows) + most(LOWER) * LAGS[LOWER] + WAITS[LOWER], strips)
     row_at = key_at + groups
     caught = 0
     while caught < blocks and per_block * (caught + 1) <= row_at + 2 * caught:
         caught += 1
-    top_at = max(row_at + 2 * caught, top_pieces + most * LAG)
+    top_at = max(row_at + 2 * caught, PACE - 1 + top_pieces + most(TOP) * LAGS[TOP] + WAITS[TOP])
     product_at = top_at + groups
-    weight_from = product_at + 2 * groups
+    weight_from = product_at + groups * groups
     column_n = depth // big
-    tile_from = offset // SPAN + most * LAG
-    last_tile = (depth - width) // SPAN + most * LAG
+    tile_from = tile_start + PACE - 1 + jnp.maximum(0, most(TILEROWS) * LAGS[TILEROWS] + wait(TILEROWS))
+    last_tile = PACE - 1 + max((depth - width) // SPAN, LATER[TILEROWS]) + most(TILEROWS) * LAGS[TILEROWS] + max(WAITS[TILEROWS], 0)
     window = 1 + column_n
     weight_starts = [
         jnp.maximum(weight_from + window * j, tile_from + per_block * (j + 1)) for j in range(groups)
@@ -504,7 +587,7 @@
             (inv_at, groups, inv_piece),
             (key_at, groups, key_piece),
             (top_at, groups, top_piece),
-            (product_at, 2 * groups, product_piece),
+            (product_at, groups * groups, product_piece),
         ):
             @pl.when(between(i, start, count))
             def _(start=start, piece=piece):
@@ -538,7 +621,7 @@
         def _():
             @pl.loop(0, pieces)
             def _(i):
-                z_copy(i, zbuf, zbuf).wait_send()
+                z_each(i, lambda source, target, columns: z_copy(i, target, target, columns).wait_send())
 
     if rows_n > 1:
         for item in range(4):
@@ -551,7 +634,7 @@
     f32, bf16 = jnp.float32, jnp.bfloat16
     tile_n = min(TILE, width)
     dma = pltpu.SemaphoreType.DMA
-    pieces, top_pieces, low_pieces = depth // SPAN, width // SPAN, width // (2 * SPAN)
+    pieces, top_pieces, low_pieces = depth // SPAN, width // (PACE * SPAN), width // (2 * PACE * SPAN)
     square = pltpu.VMEM((width, width), f32)
     narrow = pltpu.VMEM((width, width), bf16)
     return pl.pallas_call(
@@ -579,13 +662,13 @@
             pltpu.VMEM((tile_n, width), bf16),
             dma((pieces,)),
             dma((pieces,)),
-            dma((2, 2)),
-            dma((2,)),
+            dma((2, couple_parts(half))),
+            dma((couple_parts(half),)),
             dma((2, low_pieces)),
             dma((low_pieces,)),
             dma((2, top_pieces)),
             dma((top_pieces,)),
-            dma((2, top_pieces)),
+            dma((3, top_pieces)),
             dma((top_pieces,)),
             dma((3 * (depth // tile_n) + 5,)),
         ],

time: 244 us -> 211 us (0.86)
  Pallas kernels: 239 us -> 205 us
    pallas_call x1, Pallas kernels: 239 us -> 205 us  [body(): pl.pallas_call(functools.partial(step_kernel, rows_n, cols_n), out_shape=...]
where the time goes in v1:
time: 211 us; the launch traced here: 208 us
  Pallas kernels  205 us (97%)
  local copies, waits for them, and re-layouts  3.4 us (2%)
    pallas_call x1, Pallas kernels, body(): pl.pallas_call(functools.partial(step_kernel, rows_n, cols_n), out_shape=...  205 us

profile of v1, /device:TPU:27, one launch (start us, length us, event | category | flops | bytes accessed | tf_op | source)
XLA Modules:
  0.0 208.1 jit_solution(14341242891472405553)
XLA Ops:
  0.0 204.7 %shard_map.37 = f32[2048,1024]{1,0:T(8,128)S(1)} custom-call(f32[2048,1024]{1,0:T(8,128)} %a_ref.1, f32[2048,1024]{1,0:T(8,128)} %l_ref.1, f32[2,512,512]{2,1,0:T(8,128)} %i_ref.1), custom_call_target="tpu_custom_call" | custom-call | tf_op jit(solution)/shard_map/pallas_call | solution.py:640
  204.7 3.4 %copy.5 = f32[2048,1024]{1,0:T(8,128)} copy(f32[2048,1024]{1,0:T(8,128)S(1)} %shard_map.37) | data formatting | bytes 16777216

commit v2 on v1

--- a/solution.py
+++ b/solution.py
@@ -11,10 +11,12 @@
 SPAN = 16
 PACE = 2
 TILE = 256
-AHEAD = (2, 16)
+RECENT = 8
+BEHIND = 12
+AHEAD = (3, 24)
 LAGS = (4, 4, 4, 3)
 LATER = (0, 4, 0, 36)
-WAITS = (6, 6, 6, -8, -6)
+WAITS = (6, 6, 6, -10, -4)
 NN, NT = ((1,), (0,)), ((1,), (1,))
 COUPLE, LOWER, TOP, TILEROWS = range(4)
 
@@ -238,29 +240,39 @@
 
                 each(item, at, act)
 
+                if item == TILEROWS:
+                    @pl.when(jnp.logical_and(sends_on[item], at >= RECENT))
+                    def _():
+                        p_sent(item, at - RECENT)
+
+    def p_sent(item, at):
+        buffer = items[item][0]
+
+        def act(columns):
+            for way in range(2):
+                if chain > 1:
+                    @pl.when(jnp.logical_and(at % 2 == way, jnp.logical_not(is_last[item][way])))
+                    def _():
+                        p_copy(item, 0, at, buffer, 0, columns, row).wait_send()
+
+            if chain > 2 and item == TILEROWS:
+                @pl.when(is_first[item])
+                def _():
+                    p_copy(item, 2, at, buffer, 0, columns, row).wait_send()
+
+            if pair > 1:
+                p_copy(item, 1, at, buffer, 0, columns, row).wait_send()
+
+        each(item, at, act)
+
     def p_finish(item):
-        buffer, count = items[item][0], items[item][4]
+        held = RECENT if item == TILEROWS else items[item][4]
 
         @pl.when(jnp.logical_and(wanted[item], sends_on[item]))
         def _():
-            @pl.loop(0, count)
+            @pl.loop(max(0, items[item][4] - held), items[item][4])
             def _(at):
-                def act(columns):
-                    for way in range(2):
-                        if chain > 1:
-                            @pl.when(jnp.logical_and(at % 2 == way, jnp.logical_not(is_last[item][way])))
-                            def _():
-                                p_copy(item, 0, at, buffer, 0, columns, row).wait_send()
-
-                    if chain > 2 and item == TILEROWS:
-                        @pl.when(is_first[item])
-                        def _():
-                            p_copy(item, 2, at, buffer, 0, columns, row).wait_send()
-
-                    if pair > 1:
-                        p_copy(item, 1, at, buffer, 0, columns, row).wait_send()
-
-                each(item, at, act)
+                p_sent(item, at)
 
     def z_copy(i, source, target, columns):
         rows = pl.ds(pl.multiple_of(sent_at(i, top_pieces) * SPAN, SPAN), SPAN)
@@ -308,6 +320,9 @@
                     z_copy(i, target, target, columns).start()
 
             z_each(i, act)
+
+    def z_sent(i):
+        z_each(i, lambda source, target, columns: z_copy(i, target, target, columns).wait_send())
 
     def l_load(b):
         return pltpu.make_async_copy(
@@ -507,7 +522,7 @@
         ch[rows_of(b)], cl[rows_of(b)] = split(top[rows_of(b)])
 
     def product_piece(h):
-        b, group = h // groups, h % groups
+        b, group = h % groups, h // groups
         high, rest = kh.at[rows_of(b)], kl.at[rows_of(b)]
         for n in range(groups):
             own, at = slice(n * tile_n, (n + 1) * tile_n), (n + 1) * tile_n
@@ -551,19 +566,22 @@
     caught = 0
     while caught < blocks and per_block * (caught + 1) <= row_at + 2 * caught:
         caught += 1
-    top_at = max(row_at + 2 * caught, PACE - 1 + top_pieces + most(TOP) * LAGS[TOP] + WAITS[TOP])
-    product_at = top_at + groups
-    weight_from = product_at + groups * groups
+    top_from = PACE - 1 + most(TOP) * LAGS[TOP] + WAITS[TOP]
+    early_at = max(row_at + 2 * caught, top_from + per_block * (groups - 1))
+    early_n = groups * (groups - 1)
+    top_at = max(early_at + groups - 1 + early_n, top_from + top_pieces)
+    weight_from = top_at + 1 + groups
     column_n = depth // big
     tile_from = tile_start + PACE - 1 + jnp.maximum(0, most(TILEROWS) * LAGS[TILEROWS] + wait(TILEROWS))
     last_tile = PACE - 1 + max((depth - width) // SPAN, LATER[TILEROWS]) + most(TILEROWS) * LAGS[TILEROWS] + max(WAITS[TILEROWS], 0)
     window = 1 + column_n
+    apart = max(window, (pieces - weight_from - window) // groups)
     weight_starts = [
-        jnp.maximum(weight_from + window * j, tile_from + per_block * (j + 1)) for j in range(groups)
+        jnp.maximum(weight_from + apart * j, tile_from + per_block * (j + 1)) for j in range(groups)
     ]
     steps = max(
         pieces + 2,
-        max(weight_from + window * (groups - 1), last_tile + per_block * groups) + window,
+        max(weight_from + apart * (groups - 1), last_tile + per_block * groups) + window,
         top_at + groups,
     )
 
@@ -577,21 +595,36 @@
             def _():
                 z_step(i)
 
+            @pl.when(jnp.logical_and(relays, between(i, BEHIND, pieces)))
+            def _():
+                z_sent(i - BEHIND)
+
         if rows_n > 1:
             for item in range(4):
                 p_step(item, i)
+
+            @pl.when(i == top_at)
+            def _():
+                for item in (COUPLE, LOWER, TOP):
+                    p_finish(item)
 
         for start, count, piece in (
             (0, strips, l_piece),
             (corner_at, corner_n, corner_piece),
             (inv_at, groups, inv_piece),
             (key_at, groups, key_piece),
-            (top_at, groups, top_piece),
-            (product_at, groups * groups, product_piece),
         ):
             @pl.when(between(i, start, count))
             def _(start=start, piece=piece):
                 piece(i - start)
+
+        @pl.when(jnp.logical_or(between(i, early_at, groups - 1), i == top_at))
+        def _():
+            top_piece(jnp.where(i == top_at, groups - 1, i - early_at))
+
+        @pl.when(jnp.logical_or(between(i, early_at + groups - 1, early_n), between(i, top_at + 1, groups)))
+        def _():
+            product_piece(jnp.where(i > top_at, early_n + i - top_at - 1, i - early_at - groups + 1))
 
         late = i // per_block - 1
         early = between(i, row_at, 2 * caught)
@@ -619,13 +652,12 @@
     if cols_n > 1:
         @pl.when(relays)
         def _():
-            @pl.loop(0, pieces)
+            @pl.loop(max(0, steps - BEHIND), pieces)
             def _(i):
-                z_each(i, lambda source, target, columns: z_copy(i, target, target, columns).wait_send())
+                z_sent(i)
 
     if rows_n > 1:
-        for item in range(4):
-            p_finish(item)
+        p_finish(TILEROWS)
 
 
 def body(rows_n, cols_n, a_window, l_panel, l_inverse):

time: 211 us -> 207 us (0.981)
  Pallas kernels: 205 us -> 200 us
    pallas_call x1, Pallas kernels: 205 us -> 200 us  [body(): pl.pallas_call(functools.partial(step_kernel, rows_n, cols_n), out_shape=...]
where the time goes in v2:
time: 207 us; the launch traced here: 203 us
  Pallas kernels  200 us (97%)
  local copies, waits for them, and re-layouts  3.4 us (2%)
    pallas_call x1, Pallas kernels, body(): pl.pallas_call(functools.partial(step_kernel, rows_n, cols_n), out_shape=...  200 us

profile of v2, /device:TPU:27, one launch (start us, length us, event | category | flops | bytes accessed | tf_op | source)
XLA Modules:
  0.0 203.2 jit_solution(17775948305416621686)
XLA Ops:
  0.0 199.8 %shard_map.37 = f32[2048,1024]{1,0:T(8,128)S(1)} custom-call(f32[2048,1024]{1,0:T(8,128)} %a_ref.1, f32[2048,1024]{1,0:T(8,128)} %l_ref.1, f32[2,512,512]{2,1,0:T(8,128)} %i_ref.1), custom_call_target="tpu_custom_call" | custom-call | tf_op jit(solution)/shard_map/pallas_call | solution.py:672
  199.8 3.4 %copy.5 = f32[2048,1024]{1,0:T(8,128)} copy(f32[2048,1024]{1,0:T(8,128)S(1)} %shard_map.37) | data formatting | bytes 16777216

commit v3 on v2

--- a/solution.py
+++ b/solution.py
@@ -517,6 +517,18 @@
             columns = pl.ds(pl.multiple_of(side * (width // 2), width // 2), width // 2)
             high, rest = split(zbuf[rows_of(b)])
             out_ref[rows_of(b), columns] -= dot3(high, rest, kh[columns], kl[columns], NT)
+
+    fine = tile_n // 2
+
+    def last_piece(part, side):
+        first = sent_at(blocks - 1, groups) * tile_n + part * fine
+
+        @pl.when(jnp.logical_not(jnp.logical_and(row == 0, first < width)))
+        def _():
+            rows = pl.ds(pl.multiple_of(first, fine), fine)
+            columns = pl.ds(pl.multiple_of(side * (width // 2), width // 2), width // 2)
+            high, rest = split(zbuf[rows])
+            out_ref[rows, columns] -= dot3(high, rest, kh[columns], kl[columns], NT)
 
     def top_piece(b):
         ch[rows_of(b)], cl[rows_of(b)] = split(top[rows_of(b)])
@@ -628,11 +640,18 @@
 
         late = i // per_block - 1
         early = between(i, row_at, 2 * caught)
-        in_time = jnp.logical_and(i % per_block < 2, jnp.logical_and(late >= caught, late < blocks))
+        in_time = jnp.logical_and(i % per_block < 2, jnp.logical_and(late >= caught, late < blocks - 1))
 
         @pl.when(jnp.logical_or(early, in_time))
         def _():
             row_piece(jnp.where(early, i - row_at, 2 * late + i % per_block))
+
+        if caught < blocks:
+            at_first = between(i, pieces - per_block // 2, 2)
+
+            @pl.when(jnp.logical_or(at_first, between(i, pieces, 2)))
+            def _():
+                last_piece(jnp.where(at_first, 0, 1), i % 2)
 
         group, at, busy = 0, 0, 0
         for j in range(groups):

time: 207 us -> 207 us (level)
  no operation moved by 1% of the time
where the time goes in v3:
time: 207 us; the launch traced here: 204 us
  Pallas kernels  201 us (97%)
  local copies, waits for them, and re-layouts  3.4 us (2%)
    pallas_call x1, Pallas kernels, body(): pl.pallas_call(functools.partial(step_kernel, rows_n, cols_n), out_shape=...  201 us

profile of v3, /device:TPU:27, one launch (start us, length us, event | category | flops | bytes accessed | tf_op | source)
XLA Modules:
  0.0 204.1 jit_solution(8587381491010702535)
XLA Ops:
  0.0 200.7 %shard_map.37 = f32[2048,1024]{1,0:T(8,128)S(1)} custom-call(f32[2048,1024]{1,0:T(8,128)} %a_ref.1, f32[2048,1024]{1,0:T(8,128)} %l_ref.1, f32[2,512,512]{2,1,0:T(8,128)} %i_ref.1), custom_call_target="tpu_custom_call" | custom-call | tf_op jit(solution)/shard_map/pallas_call | solution.py:691
  200.7 3.4 %copy.5 = f32[2048,1024]{1,0:T(8,128)} copy(f32[2048,1024]{1,0:T(8,128)S(1)} %shard_map.37) | data formatting | bytes 16777216
